TPU v7x, 128 devices: a whole 4x4x4 slice. The times are simulated.
128 devices in a mesh: row: 16 (over x, y_lo, core), col: 8 (over y_hi, z).
Axes of the slice: x: 4, y: 4 (y_hi: 2, y_lo: 2; y = y_hi * 2 + y_lo), z: 4, core: 2. Of those that a mesh axis runs over, the one named last changes fastest.
Arguments:
- pair_in: bfloat16 [768, 768, 128], P('row', 'col'), may hold values from -6 to 6
- coords: float32 [3, 768], P(None, 'row'), may hold values from -36 to 36
- chain_ids: int32 [768], P('row'), may hold values from 0 to 3, never falling along the last dimension, each value on 1 to 384 neighbouring positions
- coord_mask: int32 [768], P('row'), may hold values 0 or 1
- gain_tri: float32 [128], replicated, may hold values from 0.1 to 1.9
- gain_sum: float32 [128], replicated, may hold values from 0.1 to 1.9
- gain_attn: float32 [128], replicated, may hold values from 0.1 to 1.9
- w_tri_in: bfloat16 [128, 640], replicated, may hold values from -0.5 to 0.5
- w_tri_out: bfloat16 [128, 128], replicated, may hold values from -0.5 to 0.5
- w_bins: float32 [36, 128], replicated, may hold values from -3 to 3
- same_chain: float32 [128], replicated, may hold values from -6 to 6
- w_query: bfloat16 [128, 128], replicated, may hold values from -8 to 8
- w_attn: bfloat16 [128, 384], replicated, may hold values from -0.5 to 0.5
- w_bias: bfloat16 [128, 4], replicated, may hold values from -0.5 to 0.5
- w_attn_out: bfloat16 [128, 128], replicated, may hold values from -0.5 to 0.5
Outputs:
- pair_out: bfloat16 [768, 768, 128], P('row', 'col')
Inputs may be any that keep to these rules, and one draw needn't show every extreme that they name: `chain_ids`: chain numbers never fall along the residues, and no chain holds more than half of them.
All inputs are finite; a program needn't handle non-finite values. No bound on the sum of `coord_mask` on one device may be relied on, other than what follows from the above.
Results may differ from a plain program's by a relative error of at most 0.02.
Values may be sent and summed in bfloat16 or wider, within the bound.
No kernel may reach another device: no remote copies, remote signals or barrier semaphores. Data moves between devices by JAX's collectives and lax.ppermute only.
A program may use at most 192 MiB of HBM per device.

v0:
```python
import math
import jax
import jax.numpy as jnp
from jax import lax
from jax.sharding import PartitionSpec as P


def joined_along(tiles, dim):
    lengths = list(tiles.shape[1:])
    lengths[dim] *= tiles.shape[0]
    return jnp.moveaxis(tiles, 0, dim).reshape(lengths)


def from_everyone(array, axis):
    copies = jnp.broadcast_to(array, (lax.axis_size(axis), *array.shape))
    return lax.all_to_all(copies, axis, split_axis=0, concat_axis=0, tiled=True)


def gather_directly(array, axis, dim):
    return joined_along(from_everyone(array, axis), dim)


def layer_norm(values, gain):
    center = values - jnp.mean(values, axis=-1, keepdims=True)
    spread = jnp.mean(center * center, axis=-1, keepdims=True)
    return center * lax.rsqrt(spread + 1e-05) * gain


def body(
    pair_in,
    coords,
    chain_ids,
    coord_mask,
    gain_tri,
    gain_sum,
    gain_attn,
    w_tri_in,
    w_tri_out,
    w_bins,
    same_chain,
    w_query,
    w_attn,
    w_bias,
    w_attn_out,
):
    n_rows = lax.axis_size("row")
    n_cols = lax.axis_size("col")
    row_count, col_count, channels = pair_in.shape
    n_heads = w_bias.shape[1]
    head_size = channels // n_heads
    n_bins = w_bins.shape[0]
    total_res = row_count * n_rows
    stride = col_count // n_rows
    col_start = lax.axis_index("col") * col_count
    coords_all, chains_all, masks_all = (
        gather_directly(coords, "row", 1),
        gather_directly(chain_ids, "row", 0),
        gather_directly(coord_mask, "row", 0),
    )
    pair_wide = pair_in.astype(jnp.float32)
    normed = layer_norm(pair_wide, gain_tri).astype(jnp.bfloat16)
    projected = jnp.dot(
        normed.reshape(row_count * col_count, channels),
        w_tri_in,
        preferred_element_type=jnp.float32,
    ).reshape(row_count, col_count, 5 * channels)
    left_side = (
        (jax.nn.sigmoid(projected[..., :channels]) * projected[..., channels : 2 * channels])
        .astype(jnp.bfloat16)
        .transpose(2, 0, 1)
    )
    right_side = (
        (
            jax.nn.sigmoid(projected[..., 2 * channels : 3 * channels])
            * projected[..., 3 * channels : 4 * channels]
        )
        .astype(jnp.bfloat16)
        .transpose(2, 0, 1)
    )
    tri_gate = jax.nn.sigmoid(projected[..., 4 * channels :])
    left_rows = lax.all_gather(left_side, "col", axis=2, tiled=True)
    left_perm = (
        left_rows.reshape(channels, row_count, n_cols, n_rows, stride)
        .transpose(0, 1, 3, 2, 4)
        .reshape(channels, row_count, total_res)
    )
    moved = lax.all_to_all(
        lax.all_to_all(right_side, "row", split_axis=2, concat_axis=1, tiled=True),
        "col",
        split_axis=1,
        concat_axis=2,
        tiled=True,
    )
    product = jnp.einsum(
        "cik,cjk->cij",
        left_perm,
        lax.all_gather(moved, "row", axis=2, tiled=True),
        preferred_element_type=jnp.float32,
    ).transpose(1, 2, 0)
    summed_norm = layer_norm(product, gain_sum).astype(jnp.bfloat16)
    pair_one = pair_wide + tri_gate * jnp.dot(
        summed_norm.reshape(row_count * col_count, channels),
        w_tri_out,
        preferred_element_type=jnp.float32,
    ).reshape(row_count, col_count, channels)
    far_coords = lax.dynamic_slice_in_dim(coords_all, col_start, col_count, 1)
    far_chains = lax.dynamic_slice_in_dim(chains_all, col_start, col_count, 0)
    far_masks = lax.dynamic_slice_in_dim(masks_all, col_start, col_count, 0)
    offsets = coords[:, :, None] - far_coords[:, None, :]
    dist = jnp.sqrt(jnp.sum(offsets * offsets, axis=0) + 1.0)
    centres = 2.0 + 20.0 * jnp.arange(n_bins, dtype=jnp.float32) / (n_bins - 1)
    spacing = 25.0 / (n_bins - 1)
    pair_mask = coord_mask.astype(jnp.float32)[:, None] * far_masks.astype(jnp.float32)[None, :]
    feats = jnp.exp(-(((dist[..., None] - centres) / spacing) ** 2)) * pair_mask[..., None]
    binned = jnp.dot(feats.reshape(row_count * col_count, n_bins), w_bins).reshape(
        row_count, col_count, channels
    )
    shared = (chain_ids[:, None] == far_chains[None, :]).astype(jnp.float32)
    pair_two = (pair_one + binned + shared[..., None] * same_chain).astype(jnp.bfloat16)
    normed_two = layer_norm(pair_two.astype(jnp.float32), gain_attn).astype(jnp.bfloat16)
    flat_two = normed_two.reshape(row_count * col_count, channels)
    queries = (
        jnp.dot(flat_two, w_query, preferred_element_type=jnp.float32)
        .astype(jnp.bfloat16)
        .reshape(row_count, col_count, n_heads, head_size)
    )
    gate_pre = jnp.dot(
        flat_two, w_attn[:, 2 * channels :], preferred_element_type=jnp.float32
    ).reshape(row_count, col_count, channels)
    attn_gate = jax.nn.sigmoid(gate_pre)
    pair_bias = (
        jnp.dot(flat_two, w_bias, preferred_element_type=jnp.float32)
        .astype(jnp.bfloat16)
        .reshape(row_count, col_count, n_heads)
        .transpose(2, 0, 1)
    )
    bias_moved = lax.all_to_all(
        lax.all_to_all(pair_bias, "row", split_axis=2, concat_axis=1, tiled=True),
        "col",
        split_axis=1,
        concat_axis=2,
        tiled=True,
    )
    bias_gathered = gather_directly(bias_moved, "row", 2)
    bias_mine = (
        bias_gathered.reshape(n_heads, col_count, n_rows, n_cols, stride)
        .transpose(0, 1, 3, 2, 4)
        .reshape(n_heads, col_count, total_res)
    )
    group = math.gcd(row_count, 8)
    blocks = row_count // group
    query_groups = queries.reshape(blocks, group, col_count, n_heads, head_size)
    root_dim = math.sqrt(head_size)
    start_state = (
        jnp.full((blocks, group, n_heads, col_count), -1e30, jnp.float32),
        jnp.zeros((blocks, group, n_heads, col_count), jnp.float32),
        jnp.zeros((blocks, group, n_heads, col_count, head_size), jnp.float32),
    )
    panel = lax.all_gather(normed_two, "col", axis=1, tiled=True)
    span = panel.shape[1]
    both = jnp.dot(
        panel.reshape(row_count * span, channels),
        w_attn[:, : 2 * channels],
        preferred_element_type=jnp.float32,
    ).reshape(row_count, span, 2 * channels)
    key_part = both[..., :channels].astype(jnp.bfloat16)
    span = key_part.shape[1]
    bias_part = bias_mine.astype(jnp.float32)
    key_groups = key_part.reshape(blocks, group, span, n_heads, head_size)
    value_groups = (
        both[..., channels:].astype(jnp.bfloat16).reshape(blocks, group, span, n_heads, head_size)
    )

    def one_block(items):
        query_blk, key_blk, value_blk, running_top, running_total, running_acc = items
        scores = (
            jnp.einsum("ijhd,ikhd->ihjk", query_blk, key_blk, preferred_element_type=jnp.float32)
            / root_dim
            + bias_part[None]
        )
        new_top = jnp.maximum(running_top, jnp.max(scores, axis=-1))
        rescale = jnp.exp(running_top - new_top)
        expo = jnp.exp(scores - new_top[..., None])
        new_total = running_total * rescale + jnp.sum(expo, axis=-1)
        new_acc = running_acc * rescale[..., None] + jnp.einsum(
            "ihjk,ikhd->ihjd",
            expo.astype(jnp.bfloat16),
            value_blk,
            preferred_element_type=jnp.float32,
        )
        return (new_top, new_total, new_acc)

    final_top, final_total, final_acc = lax.map(
        one_block,
        (query_groups, key_groups, value_groups, start_state[0], start_state[1], start_state[2]),
    )
    attended = (
        (final_acc / final_total[..., None])
        .reshape(row_count, n_heads, col_count, head_size)
        .transpose(0, 2, 1, 3)
        .reshape(row_count, col_count, channels)
    )
    gated = (attn_gate * attended).astype(jnp.bfloat16)
    result = pair_two.astype(jnp.float32) + jnp.dot(
        gated.reshape(row_count * col_count, channels),
        w_attn_out,
        preferred_element_type=jnp.float32,
    ).reshape(row_count, col_count, channels)
    return result.astype(jnp.bfloat16)


def solution(mesh):
    return jax.shard_map(
        body,
        mesh=mesh,
        in_specs=(
            P("row", "col", None),
            P(None, "row"),
            P("row"),
            P("row"),
            P(),
            P(),
            P(),
            P(),
            P(),
            P(),
            P(),
            P(),
            P(),
            P(),
            P(),
        ),
        out_specs=P("row", "col", None),
        check_vma=False,
    )
```

profile of v0, /device:TPU:0, one launch (start us, length us, event | category | flops | bytes accessed | tf_op | source)
XLA Modules:
  0.0 540.9 jit_solution(7241919329803855443)
XLA Ops:
  18.4 23.0 %all_to_all.94 = bf16[128,48,96]{0,1,2:T(8,128)(2,1)S(1)} all-to-all(bf16[128,48,96]{0,1,2:T(8,128)(2,1)S(1)} %copy.109), channel_id=1, replica_groups=mesh['row'=16,'col'=8] {'row'}, dimensions={2} | all-to-all | bytes 2359296 | tf_op jit(solution)/shard_map/all_to_all | solution.py:88
  42.3 35.2 %all_to_all.95 = bf16[128,768,6]{0,2,1:T(8,128)(2,1)S(1)} all-to-all(bf16[128,768,6]{0,2,1:T(8,128)(2,1)S(1)} %copy.111), channel_id=1, replica_groups=mesh['row'=16,'col'=8] {'col'}, dimensions={1} | all-to-all | bytes 2359296 | tf_op jit(solution)/shard_map/all_to_all | solution.py:87
  79.5 9.9 %all_to_all.96 = s32[16,1,48]{2,1,0:T(1,128)S(1)} all-to-all(s32[16,1,48]{2,1,0:T(1,128)S(1)} %broadcast_in_dim.13), channel_id=1, replica_groups=mesh['row'=16,'col'=8] {'row'}, dimensions={0} | all-to-all | bytes 6144 | tf_op jit(solution)/shard_map/all_to_all | solution.py:16
  90.0 3.4 all-to-all-start.4
  95.5 4.0 all-to-all-done.4
  99.4 3.5 all-to-all-start.2
  104.4 4.6 all-to-all-done.2
  110.7 48.2 %all-gather.4.cloned.1.call-done = bf16[128,48,768]{0,2,1:T(8,128)(2,1)} async-done(((bf16[128,48,96]{0,2,1:T(8,128)(2,1)}), bf16[128,48,768]{0,2,1:T(8,128)(2,1)}) %all-gather.4.cloned.1.call-update) | async-done | bytes 9437200 | tf_op jit(solution)/shard_map/all_gather | solution.py:81
  158.9 13.4 %copy.107 = bf16[128,48,768]{0,1,2:T(8,128)(2,1)} copy(bf16[128,48,768]{0,2,1:T(8,128)(2,1)} %all-gather.4.cloned.1.call-done) | data formatting | bytes 18874368 | tf_op jit(solution)/shard_map/all_gather | solution.py:81
  172.2 10.0 %copy.108 = bf16[128,48,16,8,6]{0,1,4,3,2:T(8,128)(2,1)} copy(bf16[128,48,16,8,6]{0,1,4,2,3:T(8,128)(2,1)} %bitcast.128) | data formatting | bytes 18874368 | tf_op jit(solution)/shard_map/transpose | solution.py:84
  182.2 14.3 %copy.115 = bf16[128,48,768]{2,1,0:T(8,128)(2,1)} copy(bf16[128,48,768]{0,1,2:T(8,128)(2,1)} %bitcast.129) | data formatting | bytes 18874368 | tf_op jit(solution)/shard_map/reshape | solution.py:85
  196.6 92.8 %all-gather.6.cloned.1.call-done = bf16[128,96,768]{1,2,0:T(8,128)(2,1)} async-done(((bf16[128,96,48]{1,2,0:T(8,128)(2,1)}), bf16[128,96,768]{1,2,0:T(8,128)(2,1)}) %all-gather.6.cloned.1.call-update) | async-done | bytes 18874384 | tf_op jit(solution)/shard_map/all_gather | solution.py:97
  289.3 13.4 %bitcast_reduce_fusion = (f32[48,96]{1,0:T(8,128)S(1)}, f32[128,48,96]{2,1,0:T(8,128)S(1)}) fusion(bf16[128,48,768]{2,1,0:T(8,128)(2,1)} %copy.115, bf16[128,96,768]{1,2,0:T(8,128)(2,1)} %all-gather.6.cloned.1.call-done), kind=kOutput, calls=%fused_computation.32 | convolution fusion | flops 906554880 | bytes 30689280 | tf_op jit(solution)/shard_map/cik,cjk->cij/dot_general | solution.py:94
  305.4 3.8 convert_reduce_fusion
  315.5 10.9 %all_to_all.97 = bf16[16,2,576]{2,1,0:T(2,128)(2,1)S(1)} all-to-all(bf16[16,2,576]{2,1,0:T(2,128)(2,1)S(1)} %reshape.272), channel_id=1, replica_groups=mesh['row'=16,'col'=8] {'row'}, dimensions={0} | all-to-all | bytes 73728 | tf_op jit(solution)/shard_map/all_to_all | solution.py:138
  328.5 14.5 %all_to_all.98 = bf16[8,2,1152]{2,1,0:T(2,128)(2,1)S(1)} all-to-all(bf16[8,2,1152]{2,1,0:T(2,128)(2,1)S(1)} %reshape.274), channel_id=1, replica_groups=mesh['row'=16,'col'=8] {'col'}, dimensions={0} | all-to-all | bytes 73728 | tf_op jit(solution)/shard_map/all_to_all | solution.py:137
  346.3 3.8 all-to-all-start.7
  353.8 10.0 %all-to-all-done.7 = bf16[16,4,96,48]{2,3,1,0:T(8,128)(2,1)S(1)} async-done(((bf16[16,4,96,48]{2,3,1,0:T(8,128)(2,1)}), bf16[16,4,96,48]{2,3,1,0:T(8,128)(2,1)S(1)}, u32[]{:S(2)}, u32[]{:S(2)}) %all-to-all-start.7) | async-done | bytes 589856 | tf_op jit(solution)/shard_map/all_to_all | solution.py:16
  365.9 64.9 %all-gather.8.cloned.1.call-done = bf16[48,768,128]{2,1,0:T(8,128)(2,1)} async-done(((bf16[48,96,128]{2,1,0:T(8,128)(2,1)}), bf16[48,768,128]{2,1,0:T(8,128)(2,1)}) %all-gather.8.cloned.1.call-update) | async-done | bytes 9437200 | tf_op jit(solution)/shard_map/all_gather | solution.py:159
  430.8 11.4 %convolution_convert_fusion = bf16[48,768,256]{1,2,0:T(8,128)(2,1)} fusion(bf16[48,768,128]{2,1,0:T(8,128)(2,1)} %all-gather.8.cloned.1.call-done, bf16[128,384]{1,0:T(8,128)(2,1)S(1)} %copy-done.7), kind=kOutput, calls=%fused_computation.22 | convolution fusion | flops 2425356288 | bytes 28377088 | tf_op jit(solution)/shard_map/dot_general | solution.py:161
  442.3 14.3 %fusion.89 = (bf16[48,768,128]{1,2,0:T(8,128)(2,1)}, bf16[48,768,128]{1,2,0:T(8,128)(2,1)}) fusion(bf16[48,768,256]{1,2,0:T(8,128)(2,1)} %convolution_convert_fusion), kind=kLoop, calls=%fused_computation.111 | loop fusion | bytes 37748736 | tf_op jit(solution)/shard_map/slice | solution.py:171
  456.6 68.5 %while.12 = (s32[]{:T(128)}, f32[6,8,4,96]{3,2,1,0:T(4,128)S(1)}, f32[6,8,4,96,32]{3,4,2,1,0:T(8,128)}, bf16[6,8,96,4,32]{2,1,0,4,3:T(8,128)(2,1)}, bf16[6,8,768...) while((s32[]{:T(128)}, f32[6,8,4,96]{3,2,1,0:T(4,128)S(1)}, ...), condition=%wide.region_10.11_spmd, body=%wide.region_7.10_spmd.sunk | while | flops 328055808 | bytes 36259420 | solution.py:193
  457.5 3.0 fusion.108
  460.6 5.0 fusion.110
  469.0 3.0 fusion.108
  472.0 5.0 fusion.110
  483.4 5.0 fusion.110
  491.8 3.0 fusion.108
  494.9 4.9 fusion.110
  506.3 5.0 fusion.110
  517.7 4.9 fusion.110
  529.7 4.4 fusion.41
  (137 shorter events, 74.7 us)
Async XLA Ops:
  6.5 4.6 copy-start
  6.5 4.6 copy-start.4
  6.5 4.6 copy-start.13
  6.5 152.3 %all-gather.4.cloned.1.call-start = ((), (), s32[]{:S(2)}) async-start(), calls=%async_computation.8 | async-start | bytes 10616832 | tf_op jit(solution)/shard_map/all_gather | solution.py:81
  13.2 4.7 copy-start.2
  17.9 271.4 %all-gather.6.cloned.1.call-start = ((), (), s32[]{:S(2)}) async-start(), calls=%async_computation.9 | async-start | bytes 26738688 | tf_op jit(solution)/shard_map/all_gather | solution.py:97
  77.7 1.8 copy-start.15
  77.7 11.7 %copy-start.11 = (s32[48]{0:T(128)S(1)}, s32[48]{0:T(128)}, u32[]{:S(2)}) copy-start(s32[48]{0:T(128)} %param.19) | copy-start | bytes 580
  77.7 15.8 %copy-start.10 = (f32[3,48]{1,0:T(4,128)S(1)}, f32[3,48]{1,0:T(4,128)}, u32[]{:S(2)}) copy-start(f32[3,48]{1,0:T(4,128)} %param.18) | copy-start | bytes 1732
  90.0 9.4 %all-to-all-start.4 = ((s32[16,1,48]{2,1,0:T(1,128)}), s32[16,1,48]{2,1,0:T(1,128)S(1)}, u32[]{:S(2)}, u32[]{:S(2)}) async-start(s32[16,1,48]{2,1,0:T(1,128)} %broadcast_in_dim.14), calls=%async_computation.4 | async-start | bytes 16384 | tf_op jit(solution)/shard_map/all_to_all | solution.py:16
  99.4 9.5 %all-to-all-start.2 = ((f32[16,1,144]{2,1,0:T(1,128)}), f32[16,1,144]{2,1,0:T(1,128)S(1)}, u32[]{:S(2)}, u32[]{:S(2)}) async-start(f32[16,1,144]{2,1,0:T(1,128)} %reshape.270), calls=%async_computation.2 | async-start | bytes 32768 | tf_op jit(solution)/shard_map/all_to_all | solution.py:16
  102.9 327.9 %all-gather.8.cloned.1.call-start = ((), (), s32[]{:S(2)}) async-start(), calls=%async_computation.10 | async-start | bytes 10616832 | tf_op jit(solution)/shard_map/all_gather | solution.py:159
  302.7 0.7 copy-start.14
  303.4 0.8 copy-start.8
  304.1 1.3 copy-start.5
  304.1 1.3 copy-start.18
  304.1 1.3 copy-start.19
  305.4 5.5 %copy-start.16 = (f32[128]{0:T(128)S(1)}, f32[128]{0:T(128)}, u32[]{:S(2)}) copy-start(f32[128]{0:T(128)} %param.23) | copy-start | bytes 1540
  309.2 1.7 copy-start.6
  309.2 4.2 copy-start.12
  327.3 22.9 %copy-start.3 = (bf16[48,96,128]{2,1,0:T(8,128)(2,1)S(1)}, bf16[48,96,128]{2,1,0:T(8,128)(2,1)}, u32[]{:S(2)}) copy-start(bf16[48,96,128]{2,1,0:T(8,128)(2,1)} %fusion.34) | copy-start | bytes 3538948
  327.3 22.9 %copy-start.9 = (bf16[128,128]{1,0:T(8,128)(2,1)S(1)}, bf16[128,128]{1,0:T(8,128)(2,1)}, u32[]{:S(2)}) copy-start(bf16[128,128]{1,0:T(8,128)(2,1)} %param.28) | copy-start | bytes 98308
  346.3 17.4 %all-to-all-start.7 = ((bf16[16,4,96,48]{2,3,1,0:T(8,128)(2,1)}), bf16[16,4,96,48]{2,3,1,0:T(8,128)(2,1)S(1)}, u32[]{:S(2)}, u32[]{:S(2)}) async-start(bf16[16,4,96,48]{2,3,1,0:T(8,128)(2,1)} %broadcast_in_dim.15), calls=%async_computation.7 | async-start | bytes 1572864 | tf_op jit(solution)/shard_map/all_to_all | solution.py:16
  364.2 66.6 %copy-start.7 = (bf16[128,384]{1,0:T(8,128)(2,1)S(1)}, bf16[128,384]{1,0:T(8,128)(2,1)}, u32[]{:S(2)}) copy-start(bf16[128,384]{1,0:T(8,128)(2,1)} %param.29) | copy-start | bytes 294916
  527.5 2.2 copy-start.17
  529.7 4.4 copy-start.1
Sparse Core Ops, SparseCore 0:
  18.0 140.8 all-gather.3
  160.5 128.7 all-gather.5
  313.5 117.2 all-gather.7
where the time goes:
time: 548 us; the launch traced here: 541 us
  waiting for transfers between devices  224 us (41%)
  blocking collectives  93.4 us (17%)
  matrix products  85.5 us (16%)
  local copies, waits for them, and re-layouts  79.8 us (15%)
  other arithmetic  32.5 us (6%)
  between operations  13.9 us (3%)
  starting transfers between devices  11.3 us (2%)
    all_gather x1, waiting for transfers between devices, body(): lax.all_gather(moved, 'row', axis=2, tiled=True)  92.8 us
    all_gather x1, waiting for transfers between devices, body(): panel = lax.all_gather(normed_two, 'col', axis=1, tiled=True)  64.9 us
    all_gather x1, waiting for transfers between devices, body(): left_rows = lax.all_gather(left_side, 'col', axis=2, tiled=True)  48.2 us
    all_to_all x1, blocking collectives, body(): lax.all_to_all(lax.all_to_all(right_side, 'row', split_axis=2, concat_axi...  35.2 us
    dot_general x6, matrix products, one_block(): jnp.einsum('ihjk,ikhd->ihjd', expo.astype(jnp.bfloat16), value_blk, prefe...  29.8 us
    all_to_all x1, blocking collectives, body(): lax.all_to_all(right_side, 'row', split_axis=2, concat_axis=1, tiled=True)  23 us
    all_to_all x3, waiting for transfers between devices, from_everyone(): return lax.all_to_all(copies, axis, split_axis=0, concat_axis=0, tiled=True)  18.5 us
    dot_general x6, matrix products, one_block(): jnp.einsum('ijhd,ikhd->ihjk', query_blk, key_blk, preferred_element_type=...  17.9 us
  transfers between devices with their start and end apart: 6, of which 6 were waited for; matrix products, arithmetic and copies ran while one was open for 11% of the time, Pallas kernels for 0%

commit v1 on v0

--- a/solution.py
+++ b/solution.py
@@ -3,6 +3,13 @@
 import jax.numpy as jnp
 from jax import lax
 from jax.sharding import PartitionSpec as P
+
+
+def gather_over(x, axis, dim):
+    size = lax.axis_size(axis)
+    blocks = jnp.stack([x for _ in range(size)])
+    blocks = lax.all_to_all(blocks, axis, split_axis=0, concat_axis=0)
+    return jnp.concatenate(blocks, axis=dim)
 
 
 def joined_along(tiles, dim):
@@ -78,7 +85,7 @@
         .transpose(2, 0, 1)
     )
     tri_gate = jax.nn.sigmoid(projected[..., 4 * channels :])
-    left_rows = lax.all_gather(left_side, "col", axis=2, tiled=True)
+    left_rows = gather_over(left_side, "col", 2)
     left_perm = (
         left_rows.reshape(channels, row_count, n_cols, n_rows, stride)
         .transpose(0, 1, 3, 2, 4)

time: 548 us -> 618 us (1.13)
  waiting for transfers between devices: 224 us -> 266 us
  local copies, waits for them, and re-layouts: 79.8 us -> 105 us
    all_to_all x0 -> x1, waiting for transfers between devices: none -> 185 us  [gather_over(): blocks = lax.all_to_all(blocks, axis, split_axis=0, concat_axis=0)]
    all_gather x1, waiting for transfers between devices: 92.8 us -> 0.01 us  [body(): lax.all_gather(moved, 'row', axis=2, tiled=True)]
    all_gather x1 -> x0, waiting for transfers between devices: 48.2 us -> none  [body(): left_rows = lax.all_gather(left_side, 'col', axis=2, tiled=True)]
    all_to_all x0 -> x1, local copies, waits for them, and re-layouts: none -> 18.2 us  [gather_over(): blocks = lax.all_to_all(blocks, axis, split_axis=0, concat_axis=0)]
    transpose x1, local copies, waits for them, and re-layouts: 9.99 us -> 25.2 us  [body(): left_perm = left_rows.reshape(channels, row_count, n_cols, n_rows, stride...]
    all_gather x1 -> x0, local copies, waits for them, and re-layouts: 13.4 us -> none  [body(): left_rows = lax.all_gather(left_side, 'col', axis=2, tiled=True)]
    all_to_all x1 -> x2, blocking collectives: 9.89 us -> 17.4 us  [from_everyone(): return lax.all_to_all(copies, axis, split_axis=0, concat_axis=0, tiled=True)]
    all_to_all x3 -> x2, waiting for transfers between devices: 18.5 us -> 16 us  [from_everyone(): return lax.all_to_all(copies, axis, split_axis=0, concat_axis=0, tiled=True)]
  transfers between devices with their start and end apart: 6 -> 5, of which waited for: 6 -> 4; matrix products, arithmetic and copies ran while one was open for 11% -> 13% of each run, Pallas kernels for 0% -> 0%
where the time goes in v1:
time: 618 us; the launch traced here: 610 us
  waiting for transfers between devices  266 us (43%)
  local copies, waits for them, and re-layouts  105 us (17%)
  blocking collectives  94.7 us (15%)
  matrix products  85.4 us (14%)
  other arithmetic  30.9 us (5%)
  between operations  14.3 us (2%)
  starting transfers between devices  12.7 us (2%)
    all_to_all x1, waiting for transfers between devices, gather_over(): blocks = lax.all_to_all(blocks, axis, split_axis=0, concat_axis=0)  185 us
    all_gather x1, waiting for transfers between devices, body(): panel = lax.all_gather(normed_two, 'col', axis=1, tiled=True)  64.9 us
    all_to_all x1, blocking collectives, body(): lax.all_to_all(lax.all_to_all(right_side, 'row', split_axis=2, concat_axi...  30.5 us
    dot_general x6, matrix products, one_block(): jnp.einsum('ihjk,ikhd->ihjd', expo.astype(jnp.bfloat16), value_blk, prefe...  29.8 us
    transpose x1, local copies, waits for them, and re-layouts, body(): left_perm = left_rows.reshape(channels, row_count, n_cols, n_rows, stride...  25.2 us
    all_to_all x1, blocking collectives, body(): lax.all_to_all(right_side, 'row', split_axis=2, concat_axis=1, tiled=True)  22.9 us
    all_to_all x1, local copies, waits for them, and re-layouts, gather_over(): blocks = lax.all_to_all(blocks, axis, split_axis=0, concat_axis=0)  18.2 us
    dot_general x6, matrix products, one_block(): jnp.einsum('ijhd,ikhd->ihjk', query_blk, key_blk, preferred_element_type=...  17.9 us
  transfers between devices with their start and end apart: 5, of which 4 were waited for; matrix products, arithmetic and copies ran while one was open for 13% of the time, Pallas kernels for 0%

profile of v1, /device:TPU:0, one launch (start us, length us, event | category | flops | bytes accessed | tf_op | source)
XLA Modules:
  0.0 609.9 jit_solution(1166910758803442428)
XLA Ops:
  14.5 3.0 copy-done.2
  18.0 22.9 %all_to_all.99 = bf16[128,48,96]{0,1,2:T(8,128)(2,1)S(1)} all-to-all(bf16[128,48,96]{0,1,2:T(8,128)(2,1)S(1)} %copy.108), channel_id=1, replica_groups=mesh['row'=16,'col'=8] {'row'}, dimensions={2} | all-to-all | bytes 2359296 | tf_op jit(solution)/shard_map/all_to_all | solution.py:95
  41.8 30.5 %all_to_all.100 = bf16[128,768,6]{0,2,1:T(8,128)(2,1)S(1)} all-to-all(bf16[128,768,6]{0,2,1:T(8,128)(2,1)S(1)} %copy.110), channel_id=1, replica_groups=mesh['row'=16,'col'=8] {'col'}, dimensions={1} | all-to-all | bytes 2359296 | tf_op jit(solution)/shard_map/all_to_all | solution.py:94
  74.4 8.6 %all_to_all.101 = s32[16,1,48]{2,1,0:T(1,128)S(1)} all-to-all(s32[16,1,48]{2,1,0:T(1,128)S(1)} %broadcast_in_dim.13), channel_id=1, replica_groups=mesh['row'=16,'col'=8] {'row'}, dimensions={0} | all-to-all | bytes 6144 | tf_op jit(solution)/shard_map/all_to_all | solution.py:23
  83.7 3.5 all-to-all-start.5
  87.3 6.0 all-to-all-done.5
  93.2 8.8 %all_to_all.102 = f32[16,1,144]{2,1,0:T(1,128)S(1)} all-to-all(f32[16,1,144]{2,1,0:T(1,128)S(1)} %reshape.272), channel_id=1, replica_groups=mesh['row'=16,'col'=8] {'row'}, dimensions={0} | all-to-all | bytes 18432 | tf_op jit(solution)/shard_map/all_to_all | solution.py:23
  102.0 5.2 stack.2
  107.3 5.1 all-to-all-start
  116.6 185.4 %all-to-all-done = bf16[8,128,48,96]{1,3,2,0:T(8,128)(2,1)} async-done(((bf16[8,128,48,96]{1,3,2,0:T(8,128)(2,1)}), bf16[8,128,48,96]{1,3,2,0:T(8,128)(2,1)}, u32[]{:S(2)}, u32[]{:S(2)}) %all-to-all-start) | async-done | bytes 9437216 | tf_op jit(solution)/shard_map/all_to_all | solution.py:11
  302.1 18.2 %copy.106 = bf16[8,128,48,96]{1,0,3,2:T(8,128)(2,1)} copy(bf16[8,128,48,96]{1,3,2,0:T(8,128)(2,1)} %all-to-all-done) | data formatting | bytes 18874368 | tf_op jit(solution)/shard_map/all_to_all | solution.py:11
  320.3 25.2 %copy.107 = bf16[128,48,16,8,6]{0,1,4,3,2:T(8,128)(2,1)} copy(bf16[128,48,16,8,6]{0,3,4,2,1:T(8,128)(2,1)} %bitcast.130) | data formatting | bytes 18874368 | tf_op jit(solution)/shard_map/transpose | solution.py:91
  345.5 14.0 %copy.114 = bf16[128,48,768]{2,1,0:T(8,128)(2,1)} copy(bf16[128,48,768]{0,1,2:T(8,128)(2,1)} %bitcast.131) | data formatting | bytes 18874368 | tf_op jit(solution)/shard_map/reshape | solution.py:92
  359.5 13.4 %bitcast_reduce_fusion = (f32[48,96]{1,0:T(8,128)S(1)}, f32[128,48,96]{2,1,0:T(8,128)S(1)}) fusion(bf16[128,48,768]{2,1,0:T(8,128)(2,1)} %copy.114, bf16[128,96,768]{1,2,0:T(8,128)(2,1)} %all-gather.3.cloned.1.call-done), kind=kOutput, calls=%fused_computation.32 | convolution fusion | flops 906554880 | bytes 30689280 | tf_op jit(solution)/shard_map/cik,cjk->cij/dot_general | solution.py:101
  375.5 3.8 convert_reduce_fusion
  385.7 10.0 %all_to_all.103 = bf16[16,2,576]{2,1,0:T(2,128)(2,1)S(1)} all-to-all(bf16[16,2,576]{2,1,0:T(2,128)(2,1)S(1)} %reshape.274), channel_id=1, replica_groups=mesh['row'=16,'col'=8] {'row'}, dimensions={0} | all-to-all | bytes 73728 | tf_op jit(solution)/shard_map/all_to_all | solution.py:145
  397.8 13.8 %all_to_all.104 = bf16[8,2,1152]{2,1,0:T(2,128)(2,1)S(1)} all-to-all(bf16[8,2,1152]{2,1,0:T(2,128)(2,1)S(1)} %reshape.276), channel_id=1, replica_groups=mesh['row'=16,'col'=8] {'col'}, dimensions={0} | all-to-all | bytes 73728 | tf_op jit(solution)/shard_map/all_to_all | solution.py:144
  414.9 3.8 all-to-all-start.8
  422.3 10.0 %all-to-all-done.8 = bf16[16,4,96,48]{2,3,1,0:T(8,128)(2,1)S(1)} async-done(((bf16[16,4,96,48]{2,3,1,0:T(8,128)(2,1)}), bf16[16,4,96,48]{2,3,1,0:T(8,128)(2,1)S(1)}, u32[]{:S(2)}, u32[]{:S(2)}) %all-to-all-start.8) | async-done | bytes 589856 | tf_op jit(solution)/shard_map/all_to_all | solution.py:23
  434.5 64.9 %all-gather.5.cloned.1.call-done = bf16[48,768,128]{2,1,0:T(8,128)(2,1)} async-done(((bf16[48,96,128]{2,1,0:T(8,128)(2,1)}), bf16[48,768,128]{2,1,0:T(8,128)(2,1)}) %all-gather.5.cloned.1.call-update) | async-done | bytes 9437200 | tf_op jit(solution)/shard_map/all_gather | solution.py:166
  499.4 11.4 %convolution_convert_fusion = bf16[48,768,256]{1,2,0:T(8,128)(2,1)} fusion(bf16[48,768,128]{2,1,0:T(8,128)(2,1)} %all-gather.5.cloned.1.call-done, bf16[128,384]{1,0:T(8,128)(2,1)S(1)} %copy-done.7), kind=kOutput, calls=%fused_computation.22 | convolution fusion | flops 2425356288 | bytes 28377088 | tf_op jit(solution)/shard_map/dot_general | solution.py:168
  510.8 14.3 %fusion.89 = (bf16[48,768,128]{1,2,0:T(8,128)(2,1)}, bf16[48,768,128]{1,2,0:T(8,128)(2,1)}) fusion(bf16[48,768,256]{1,2,0:T(8,128)(2,1)} %convolution_convert_fusion), kind=kLoop, calls=%fused_computation.111 | loop fusion | bytes 37748736 | tf_op jit(solution)/shard_map/slice | solution.py:178
  525.1 68.5 %while.12 = (s32[]{:T(128)}, f32[6,8,4,96]{3,2,1,0:T(4,128)S(1)}, f32[6,8,4,96,32]{3,4,2,1,0:T(8,128)}, bf16[6,8,96,4,32]{2,1,0,4,3:T(8,128)(2,1)}, bf16[6,8,768...) while((s32[]{:T(128)}, f32[6,8,4,96]{3,2,1,0:T(4,128)S(1)}, ...), condition=%wide.region_10.11_spmd, body=%wide.region_7.10_spmd.sunk | while | flops 328055808 | bytes 36259420 | solution.py:200
  526.1 3.0 fusion.108
  529.1 5.0 fusion.110
  537.5 3.0 fusion.108
  540.5 5.0 fusion.110
  552.0 5.0 fusion.110
  563.4 5.0 fusion.110
  574.8 5.0 fusion.110
  586.2 5.0 fusion.110
  598.3 4.4 fusion.41
  (136 shorter events, 73.3 us)
Async XLA Ops:
  6.5 4.6 copy-start
  6.5 4.6 copy-start.4
  6.5 4.6 copy-start.13
  6.5 352.9 %all-gather.3.cloned.1.call-start = ((), (), s32[]{:S(2)}) async-start(), calls=%async_computation.9 | async-start | bytes 26738688 | tf_op jit(solution)/shard_map/all_gather | solution.py:104
  13.2 4.3 copy-start.2
  72.6 1.8 copy-start.15
  72.6 10.5 %copy-start.11 = (s32[48]{0:T(128)S(1)}, s32[48]{0:T(128)}, u32[]{:S(2)}) copy-start(s32[48]{0:T(128)} %param.19) | copy-start | bytes 580
  72.6 14.6 %copy-start.10 = (f32[3,48]{1,0:T(4,128)S(1)}, f32[3,48]{1,0:T(4,128)}, u32[]{:S(2)}) copy-start(f32[3,48]{1,0:T(4,128)} %param.18) | copy-start | bytes 1732
  83.7 9.6 %all-to-all-start.5 = ((s32[16,1,48]{2,1,0:T(1,128)}), s32[16,1,48]{2,1,0:T(1,128)S(1)}, u32[]{:S(2)}, u32[]{:S(2)}) async-start(s32[16,1,48]{2,1,0:T(1,128)} %broadcast_in_dim.14), calls=%async_computation.5 | async-start | bytes 16384 | tf_op jit(solution)/shard_map/all_to_all | solution.py:23
  107.3 194.8 %all-to-all-start = ((bf16[8,128,48,96]{1,3,2,0:T(8,128)(2,1)}), bf16[8,128,48,96]{1,3,2,0:T(8,128)(2,1)}, u32[]{:S(2)}, u32[]{:S(2)}) async-start(bf16[8,128,48,96]{1,3,2,0:T(8,128)(2,1)} %stack.2), calls=%async_computation | async-start | bytes 18874368 | tf_op jit(solution)/shard_map/all_to_all | solution.py:11
  112.4 387.0 %all-gather.5.cloned.1.call-start = ((), (), s32[]{:S(2)}) async-start(), calls=%async_computation.10 | async-start | bytes 10616832 | tf_op jit(solution)/shard_map/all_gather | solution.py:166
  372.9 0.7 copy-start.14
  373.5 0.8 copy-start.8
  374.3 1.3 copy-start.5
  374.3 1.3 copy-start.18
  374.3 1.3 copy-start.19
  375.5 5.5 copy-start.16
  379.3 1.7 copy-start.6
  379.3 4.2 copy-start.12
  396.6 22.2 %copy-start.3 = (bf16[48,96,128]{2,1,0:T(8,128)(2,1)S(1)}, bf16[48,96,128]{2,1,0:T(8,128)(2,1)}, u32[]{:S(2)}) copy-start(bf16[48,96,128]{2,1,0:T(8,128)(2,1)} %fusion.34) | copy-start | bytes 3538948
  396.6 22.2 %copy-start.9 = (bf16[128,128]{1,0:T(8,128)(2,1)S(1)}, bf16[128,128]{1,0:T(8,128)(2,1)}, u32[]{:S(2)}) copy-start(bf16[128,128]{1,0:T(8,128)(2,1)} %param.28) | copy-start | bytes 98308
  414.9 17.4 %all-to-all-start.8 = ((bf16[16,4,96,48]{2,3,1,0:T(8,128)(2,1)}), bf16[16,4,96,48]{2,3,1,0:T(8,128)(2,1)S(1)}, u32[]{:S(2)}, u32[]{:S(2)}) async-start(bf16[16,4,96,48]{2,3,1,0:T(8,128)(2,1)} %broadcast_in_dim.15), calls=%async_computation.8 | async-start | bytes 1572864 | tf_op jit(solution)/shard_map/all_to_all | solution.py:23
  432.8 66.6 %copy-start.7 = (bf16[128,384]{1,0:T(8,128)(2,1)S(1)}, bf16[128,384]{1,0:T(8,128)(2,1)}, u32[]{:S(2)}) copy-start(bf16[128,384]{1,0:T(8,128)(2,1)} %param.29) | copy-start | bytes 294916
  596.1 2.2 copy-start.17
  598.3 4.4 copy-start.1
Sparse Core Ops, SparseCore 0:
  74.5 212.1 all-gather.2
  383.7 115.6 all-gather.4
